TPU v7x, 128 devices: a whole 4x4x4 slice. The times are simulated.
128 devices in a mesh: gx: 16 (over x, z), gy: 8 (over y, core).
Axes of the slice: x: 4, y: 4, z: 4, core: 2. Of those that a mesh axis runs over, the one named last changes fastest.
Arguments:
- velocity: float32 [3, 256, 512, 256], P(None, 'gx', 'gy'), may hold values from -6 to 6
Outputs:
- details_one: float32 [7, 9, 128, 256, 128], P(None, None, 'gx', 'gy')
- stress_one: float32 [6, 128, 256, 128], P(None, 'gx', 'gy')
- details_two: float32 [7, 9, 64, 128, 64], P(None, None, 'gx', 'gy')
- stress_two: float32 [6, 64, 128, 64], P(None, 'gx', 'gy')
- details_three: float32 [7, 9, 32, 64, 32], P(None, None, 'gx', 'gy')
- stress_three: float32 [6, 32, 64, 32], P(None, 'gx', 'gy')
- coarse_velocity: float32 [3, 32, 64, 32], P(None, 'gx', 'gy')
All inputs are finite; a program needn't handle non-finite values.
Results may differ from a plain program's by a relative error of at most 0.0003.
Values sent between devices are 32-bit elements; how exact they have to be, the bound alone decides.
A program may use at most 256 MiB of HBM per device.

v0:
```python
import jax
import jax.numpy as jnp
import numpy as np
from jax import lax
from jax.experimental import pallas as pl
from jax.experimental.pallas import tpu as pltpu
from jax.sharding import PartitionSpec as P

MESH = pl.DeviceIdType.MESH
F32 = jnp.float32
BF16 = jnp.bfloat16

predict_one = -1.586134342
update_one = -0.05298011854
predict_two = 0.8829110762
update_two = 0.4435068522
scaling = 1.149604398
product_pairs = ((0, 0), (0, 1), (0, 2), (1, 1), (1, 2), (2, 2))


def third_table(length, rows):
    identity = np.eye(length)
    even, odd = identity[:, 0::2], identity[:, 1::2]

    def ahead(values):
        return np.concatenate([values[:, 1:], values[:, -1:]], axis=1)

    def behind(values):
        return np.concatenate([values[:, :1], values[:, :-1]], axis=1)

    odd = odd + predict_one * (even + ahead(even))
    even = even + update_one * (odd + behind(odd))
    odd = odd + predict_two * (even + ahead(even))
    even = even + update_two * (odd + behind(odd))
    table = np.zeros((rows, 256))
    table[:length, : length // 2] = even * scaling
    table[:length, 128 : 128 + length // 2] = odd / scaling
    one = table.astype(np.float32).astype(BF16)
    two = (table - one.astype(np.float64)).astype(np.float32).astype(BF16)
    three = (table - one.astype(np.float64) - two.astype(np.float64)).astype(np.float32).astype(BF16)
    return np.concatenate([one, two, one, two, three, one], axis=0)


class Lift:
    def __init__(self, cell):
        self.cell = cell
        self.known = {}

    def get(self, key, make):
        if key not in self.known:
            self.known[key] = make()
        return self.known[key]

    def even(self, i):
        return self.get(("e", i), lambda: self.cell(2 * i))

    def odd(self, i):
        return self.get(("o", i), lambda: self.cell(2 * i + 1))

    def odd_one(self, i):
        return self.get(("o1", i), lambda: self.odd(i) + predict_one * (self.even(i) + self.even(i + 1)))

    def even_one(self, i):
        return self.get(("e1", i), lambda: self.even(i) + update_one * (self.odd_one(i - 1) + self.odd_one(i)))

    def high(self, i):
        return self.get(("o2", i), lambda: self.odd_one(i) + predict_two * (self.even_one(i) + self.even_one(i + 1)))

    def low(self, i):
        return self.get(("e2", i), lambda: self.even_one(i) + update_two * (self.high(i - 1) + self.high(i)))


def loop(count, body):
    def step(i, carry):
        body(i)
        return carry

    lax.fori_loop(0, count, step, 0)


def split_store(target, row, lane, value):
    one = value.astype(BF16)
    rest = value - one.astype(F32)
    two = rest.astype(BF16)
    three = (rest - two.astype(F32)).astype(BF16)
    rows = pl.ds(row, 16)
    target[0, rows, lane : lane + 128] = one
    target[1, rows, lane : lane + 128] = two
    target[2, rows, lane : lane + 128] = three


def along_y(load, block, x_high, store):
    lift = Lift(load)
    half = block // 2
    values = []
    for i in range(half):
        value = lift.low(i)
        values.append(value if x_high else value * (scaling * scaling))
    for i in range(half):
        value = lift.high(i)
        values.append(value * (1.0 / (scaling * scaling)) if x_high else value)
    for n in range(0, block, 2):
        store(n * 8, jnp.concatenate([values[n], values[n + 1]], axis=0))


def along_z(split, table, row, rows):
    at = pl.ds(row, rows)
    one, two, three = split[0, at, :], split[1, at, :], split[2, at, :]
    left = jnp.concatenate([one, one, two, two, one, three], axis=1)
    return jnp.dot(left, table[...], preferred_element_type=F32)


def kernel(count_x, count_y, v, t1, t2, t3, d1, s1, d2, s2, d3, s3, coarse,
           cells, bands, split, second, third, last, stage, w1, w2, w3,
           cs1, cr1, cs2, cr2, cs3, cr3, bands_low, split_low, own_sem, send_sem, recv_sem):
    gx, gy = lax.axis_index("gx"), lax.axis_index("gy")
    right, left = lax.rem(gx + 1, count_x), lax.rem(gx + count_x - 1, count_x)
    up, down = lax.rem(gy + 1, count_y), lax.rem(gy + count_y - 1, count_y)
    corners = ((right, up), (right, down), (left, up), (left, down))
    around = ((right, gy), (left, gy), (gx, up), (gx, down)) + corners

    own = [pltpu.make_async_copy(v.at[c], cells.at[c, 4:20, 8:72, :], own_sem.at[c]) for c in range(3)]
    tables = [pltpu.make_async_copy(src, dst, own_sem.at[3 + n]) for n, (src, dst) in enumerate(((t1, w1), (t2, w2), (t3, w3)))]
    for copy in own:
        copy.start()
    barrier = pltpu.get_barrier_semaphore()
    for device in around:
        pl.semaphore_signal(barrier, inc=1, device_id=device, device_id_type=MESH)
    for copy in tables:
        copy.start()
    pl.semaphore_wait(barrier, 8)

    started = []

    def send(src, dst, device):
        n = len(started)
        copy = pltpu.make_async_remote_copy(
            src_ref=src, dst_ref=dst, send_sem=send_sem.at[n], recv_sem=recv_sem.at[n], device_id=device, device_id_type=MESH
        )
        copy.start()
        started.append(copy)
        return copy

    def send_x(c):
        return (
            send(v.at[c, 12:16], cells.at[c, 0:4, 8:72, :], (right, gy)),
            send(v.at[c, 0:3], cells.at[c, 20:23, 8:72, :], (left, gy)),
        )

    x_halo = [send_x(0)]
    y_halo = (
        send(v.at[:, :, 56:64, :], cells.at[0:3, 4:20, 0:8, :], (gx, up)),
        send(v.at[:, :, 0:8, :], cells.at[0:3, 4:20, 72:80, :], (gx, down)),
    )
    for copy in own:
        copy.wait()
    for k, (layer, row) in enumerate(((16, 68), (16, 8), (4, 68), (4, 8))):
        for c in range(3):
            for m in range(2):
                for u in range(2):
                    cs1[k, c, m, 4 * u : 4 * u + 4, :] = cells[c, layer + 2 * m + u, row : row + 4, :]

    def fill(i):
        cells[3, i] = jnp.ones((80, 256), F32)

    loop(23, fill)
    corner_halo = [send(cs1.at[k], cr1.at[k], corners[k]) for k in range(4)]
    x_halo += [send_x(1), send_x(2)]
    for copy in tables:
        copy.wait()
    for copy in y_halo:
        copy.wait_recv()

    def level_one(g, lows, highs):
        wanted = [(0, k) for k in lows] + [(1, k) for k in highs]

        def field(t):
            other = lax.rem(t + 3, 4)
            index = 3 + lax.div((t + 1) * (6 - t), 2) + g - (6 - t)

            def along_x(i):
                rows = pl.ds(pl.multiple_of(i * 8, 8), 8)
                for h in range(2):
                    lanes = slice(128 * h, 128 * h + 128)
                    lift = Lift(lambda n: cells[g, 4 + n, rows, lanes] * cells[other, 4 + n, rows, lanes])
                    for n, (x_high, k) in enumerate(wanted):
                        bands[n, h, rows, :] = lift.high(k) if x_high else lift.low(k)

            loop(10, along_x)

            def y_band(x_high):
                def one(n):
                    n = n + len(lows) if x_high else n
                    for h in range(2):
                        along_y(
                            lambda r: bands[n, h, pl.ds(8 + r, 8, stride=8), :],
                            8,
                            x_high,
                            lambda at, value: split_store(split, pl.multiple_of(n * 64 + at, 16), 128 * h, value),
                        )

                return one

            loop(len(lows), y_band(0))
            loop(len(highs), y_band(1))
            for n, (x_high, k) in enumerate(wanted):
                out = along_z(split, w1, n * 64, 64)
                for y_high in range(2):
                    for j in range(4):
                        at = y_high * 32 + j * 8
                        for z_high in range(2):
                            value = out[at : at + 8, 128 * z_high : 128 * z_high + 128]
                            band = 4 * z_high + 2 * y_high + x_high
                            if band:
                                d1[band - 1, index, k, pl.ds(j, 8, stride=4), :] = value
                            else:
                                second[index, k, pl.ds(8 + j, 8, stride=4), :] = value

        loop(g + 2, field)

    for g in range(3):
        level_one(g, (2, 3, 4, 5), (1, 2, 3, 4, 5))
    for g in range(3):
        for copy in x_halo[g]:
            copy.wait_recv()
        if g == 0:
            for copy in corner_halo:
                copy.wait_recv()
            for k, (layer, row) in enumerate(((0, 4), (0, 72), (20, 4), (20, 72))):
                for c in range(3):
                    for m in range(2):
                        for u in range(2):
                            if layer + 2 * m + u < 23:
                                cells[c, layer + 2 * m + u, row : row + 4, :] = cr1[k, c, m, 4 * u : 4 * u + 4, :]
        level_one(g, (0, 1, 6, 7), (0, 6, 7))

    def exchange(field, n, rows, cs, cr):
        def prepare(f):
            def tile(i):
                at = pl.ds(pl.multiple_of(8 + i * 8, 8), 8)
                layer = lambda l: field[f, l, at, :]
                field[f, n + 4, at, :] = layer(n - 1) + predict_one * layer(n - 2)
                before = layer(n - 3) + predict_one * (layer(n - 4) + layer(n - 2))
                field[f, n + 5, at, :] = layer(n - 2) + update_one * before
                field[f, n + 6, at, :] = layer(0)
                field[f, n + 7, at, :] = layer(1) + predict_one * (layer(0) + layer(2))

            for i in range(rows // 8):
                tile(i)
            for k, (layer, row) in enumerate(((n + 4, 4 + rows), (n + 4, 8), (n + 6, 4 + rows), (n + 6, 8))):
                for u in range(2):
                    cs[k, f, 4 * u : 4 * u + 4, :] = field[f, layer + u, row : row + 4, :]

        loop(9, prepare)
        whole = slice(8, 8 + rows)
        halo = [
            send(field.at[:, n + 4 : n + 6, whole, :], field.at[:, n : n + 2, whole, :], (right, gy)),
            send(field.at[:, n + 6 : n + 8, whole, :], field.at[:, n + 2 : n + 4, whole, :], (left, gy)),
        ]
        halo += [send(cs.at[k], cr.at[k], corners[k]) for k in range(4)]
        halo += [
            send(field.at[:, 0:n, rows : rows + 8, :], field.at[:, 0:n, 0:8, :], (gx, up)),
            send(field.at[:, 0:n, 8:16, :], field.at[:, 0:n, 8 + rows : 16 + rows, :], (gx, down)),
        ]

        def finish():
            for copy in halo:
                copy.wait_recv()

            def unpack(f):
                for k, (layer, row) in enumerate(((n, 4), (n, 8 + rows), (n + 2, 4), (n + 2, 8 + rows))):
                    for u in range(2):
                        field[f, layer + u, row : row + 4, :] = cr[k, f, 4 * u : 4 * u + 4, :]

            loop(9, unpack)

        return finish

    def stresses(target, field, n, at):
        def layer(l):
            for k, (p, q) in enumerate(product_pairs):
                value = field[3 + k, l, at, :] - field[p, l, at, :] * field[q, l, at, :]
                target[k, l] = value[:, : target.shape[3]]

        loop(n, layer)

    def level(field, n, rows, table, put):
        half = n // 2
        block = rows // 8

        def one_field(f):
            def along_x(i):
                at = pl.ds(pl.multiple_of(i * 8, 8), 8)
                lift = Lift(lambda l: field[f, l if l < n else n + 2, at, :])
                lift.known[("o1", -1)] = field[f, n, at, :] + predict_one * lift.even(0)
                lift.known[("e1", -1)] = field[f, n + 1, at, :] + update_one * lift.odd_one(-1)
                lift.known[("o1", half)] = field[f, n + 3, at, :]
                lift.known[("o2", -1)] = lift.odd_one(-1) + predict_two * (lift.even_one(-1) + lift.even_one(0))
                for k in range(half):
                    bands_low[k, at, :] = lift.low(k)
                    bands_low[half + k, at, :] = lift.high(k)

            loop(rows // 8 + 2, along_x)

            def y_band(x_high):
                def one(k):
                    k = k + half if x_high else k
                    along_y(
                        lambda r: bands_low[k, pl.ds(8 + r, 8, stride=block), :],
                        block,
                        x_high,
                        lambda at, value: split_store(split_low, pl.multiple_of(k * rows + at, 16), 0, value),
                    )

                return one

            loop(half, y_band(0))
            loop(half, y_band(1))
            out = along_z(split_low, table, 0, n * rows)
            for k in range(n):
                x_high, x_at = divmod(k, half)
                for y_high in range(2):
                    for j in range(block // 2):
                        at = k * rows + y_high * (rows // 2) + j * 8
                        for z_high in range(2):
                            value = out[at : at + 8, 128 * z_high : 128 * z_high + 128]
                            put(f, 4 * z_high + 2 * y_high + x_high, x_at, j, value)

        loop(9, one_field)

    finish = exchange(second, 8, 32, cs2, cr2)
    stresses(s1, second, 8, slice(8, 40))
    finish()

    def put_two(f, band, k, j, value):
        if band:
            stage[band - 1, k, pl.ds(j, 8, stride=2), :] = value
            if j == 1:
                d2[band - 1, f, k] = stage[band - 1, k][:, :64]
        else:
            third[f, k, pl.ds(8 + j, 8, stride=2), :] = value

    level(second, 8, 32, w2, put_two)
    finish = exchange(third, 4, 16, cs3, cr3)
    stresses(s2, third, 4, slice(8, 24))
    finish()

    def put_three(f, band, k, j, value):
        if band:
            d3[band - 1, f, k] = value[:, :32]
        else:
            last[f, k] = value

    level(third, 4, 16, w3, put_three)
    stresses(s3, last, 2, slice(0, 8))
    for c in range(3):
        coarse[c] = last[c][:, :, :32]
    for copy in started:
        copy.wait_send()


def body(velocity):
    shapes = ((7, 9, 8, 32, 128), (6, 8, 32, 128), (7, 9, 4, 16, 64), (6, 4, 16, 64), (7, 9, 2, 8, 32), (6, 2, 8, 32), (3, 2, 8, 32))
    copies = 12 + 8 + 8
    run = pl.pallas_call(
        lambda *refs: kernel(lax.axis_size("gx"), lax.axis_size("gy"), *refs),
        out_shape=[jax.ShapeDtypeStruct(shape, F32) for shape in shapes],
        in_specs=[pl.BlockSpec(memory_space=pltpu.HBM)] * 4,
        out_specs=[pl.BlockSpec(memory_space=pltpu.VMEM)] * 7,
        scratch_shapes=[
            pltpu.VMEM((4, 23, 80, 256), F32),
            pltpu.VMEM((9, 2, 80, 128), F32),
            pltpu.VMEM((3, 576, 256), BF16),
            pltpu.VMEM((9, 16, 48, 128), F32),
            pltpu.VMEM((9, 12, 32, 128), F32),
            pltpu.VMEM((9, 2, 8, 128), F32),
            pltpu.VMEM((7, 4, 16, 128), F32),
            pltpu.VMEM((1536, 256), BF16),
            pltpu.VMEM((768, 256), BF16),
            pltpu.VMEM((768, 256), BF16),
            pltpu.VMEM((4, 3, 2, 8, 256), F32),
            pltpu.VMEM((4, 3, 2, 8, 256), F32),
            pltpu.VMEM((4, 9, 8, 128), F32),
            pltpu.VMEM((4, 9, 8, 128), F32),
            pltpu.VMEM((4, 9, 8, 128), F32),
            pltpu.VMEM((4, 9, 8, 128), F32),
            pltpu.VMEM((8, 48, 128), F32),
            pltpu.VMEM((3, 256, 128), BF16),
            pltpu.SemaphoreType.DMA((6,)),
            pltpu.SemaphoreType.DMA((copies,)),
            pltpu.SemaphoreType.DMA((copies,)),
        ],
        compiler_params=pltpu.CompilerParams(collective_id=0, has_side_effects=True, vmem_limit_bytes=34 << 20),
    )
    return tuple(run(velocity, third_table(256, 256), third_table(128, 128), third_table(64, 128)))


def solution(mesh):
    in_specs = (P(None, "gx", "gy", None),)
    out_specs = (
        P(None, None, "gx", "gy", None),
        P(None, "gx", "gy", None),
        P(None, None, "gx", "gy", None),
        P(None, "gx", "gy", None),
        P(None, None, "gx", "gy", None),
        P(None, "gx", "gy", None),
        P(None, "gx", "gy", None),
    )
    return jax.shard_map(body, mesh=mesh, in_specs=in_specs, out_specs=out_specs, check_vma=False)
```

profile of v0, /device:TPU:1, one launch (start us, length us, event | category | flops | bytes accessed | tf_op | source)
XLA Modules:
  0.0 97.5 jit_solution(18410919484222049395)
XLA Ops:
  0.6 0.0 copy-start
  0.6 1.9 %copy-done = f32[3,16,64,256]{3,2,1,0:T(8,128)S(1)} copy-done((f32[3,16,64,256]{3,2,1,0:T(8,128)S(1)}, f32[3,16,64,256]{3,2,1,0:T(8,128)}, u32[]{:S(2)}) %copy-start) | copy-done | bytes 3145752
  2.5 0.0 copy-start.1
  2.5 1.1 %copy-done.1 = bf16[1536,256]{1,0:T(8,128)(2,1)S(1)} copy-done((bf16[1536,256]{1,0:T(8,128)(2,1)S(1)}, bf16[1536,256]{1,0:T(8,128)(2,1)}, u32[]{:S(2)}) %copy-start.1) | copy-done | bytes 786456
  3.7 0.0 copy-start.2
  3.7 1.0 %copy-done.2 = bf16[768,256]{1,0:T(8,128)(2,1)S(1)} copy-done((bf16[768,256]{1,0:T(8,128)(2,1)S(1)}, bf16[768,256]{1,0:T(8,128)(2,1)}, u32[]{:S(2)}) %copy-start.2) | copy-done | bytes 393240
  4.7 0.0 copy-start.3
  4.7 1.0 %copy-done.3 = bf16[768,256]{1,0:T(8,128)(2,1)S(1)} copy-done((bf16[768,256]{1,0:T(8,128)(2,1)S(1)}, bf16[768,256]{1,0:T(8,128)(2,1)}, u32[]{:S(2)}) %copy-start.3) | copy-done | bytes 393240
  5.6 83.6 %shard_map.99 = (f32[7,9,8,32,128]{4,3,2,1,0:T(8,128)S(1)}, f32[6,8,32,128]{3,2,1,0:T(8,128)S(1)}, f32[7,9,4,16,64]{4,3,2,1,0:T(8,128)S(1)}, f32[6,4,16,64]{3,2,...) custom-call(f32[3,16,64,256]{3,2,1,0:T(8,128)S(1)} %copy-done, ...), custom_call_target="tpu_custom_call" | custom-call | tf_op jit(solution)/shard_map/pallas_call | solution.py:395
  89.2 3.4 %copy.18 = f32[7,9,8,32,128]{4,3,2,1,0:T(8,128)} copy(f32[7,9,8,32,128]{4,3,2,1,0:T(8,128)S(1)} %get-tuple-element.14) | data formatting | bytes 16515072
  92.6 0.9 copy.19
  93.5 1.3 %copy.20 = f32[7,9,4,16,64]{4,3,2,1,0:T(8,128)} copy(f32[7,9,4,16,64]{4,3,2,1,0:T(8,128)S(1)} %get-tuple-element.16) | data formatting | bytes 2064384
  94.8 0.7 copy.21
  95.4 0.8 copy.22
  96.2 0.6 copy.23
  96.8 0.6 copy.24
Async XLA Ops:
  0.6 1.9 %copy-start = (f32[3,16,64,256]{3,2,1,0:T(8,128)S(1)}, f32[3,16,64,256]{3,2,1,0:T(8,128)}, u32[]{:S(2)}) copy-start(f32[3,16,64,256]{3,2,1,0:T(8,128)} %refs_0_.1) | copy-start | bytes 9437188
  2.5 1.1 %copy-start.1 = (bf16[1536,256]{1,0:T(8,128)(2,1)S(1)}, bf16[1536,256]{1,0:T(8,128)(2,1)}, u32[]{:S(2)}) copy-start(bf16[1536,256]{1,0:T(8,128)(2,1)} %constant.6.clone.refs_1_) | copy-start | bytes 2359300
  3.7 1.0 %copy-start.2 = (bf16[768,256]{1,0:T(8,128)(2,1)S(1)}, bf16[768,256]{1,0:T(8,128)(2,1)}, u32[]{:S(2)}) copy-start(bf16[768,256]{1,0:T(8,128)(2,1)} %constant.8.clone.refs_3_) | copy-start | bytes 1179652
  4.7 1.0 %copy-start.3 = (bf16[768,256]{1,0:T(8,128)(2,1)S(1)}, bf16[768,256]{1,0:T(8,128)(2,1)}, u32[]{:S(2)}) copy-start(bf16[768,256]{1,0:T(8,128)(2,1)} %constant.7.clone.refs_2_) | copy-start | bytes 1179652
where the time goes:
time: 97.7 us; the launch traced here: 97.5 us
  Pallas kernels  83.6 us (86%)
  local copies, waits for them, and re-layouts  13.2 us (14%)
    pallas_call x1, Pallas kernels, body(): run(velocity, third_table(256, 256), third_table(128, 128), third_table(6...  83.6 us
    unnamed x15, local copies, waits for them, and re-layouts  13.2 us

commit v1 on v0

--- a/solution.py
+++ b/solution.py
@@ -37,8 +37,7 @@
     table[:length, 128 : 128 + length // 2] = odd / scaling
     one = table.astype(np.float32).astype(BF16)
     two = (table - one.astype(np.float64)).astype(np.float32).astype(BF16)
-    three = (table - one.astype(np.float64) - two.astype(np.float64)).astype(np.float32).astype(BF16)
-    return np.concatenate([one, two, one, two, three, one], axis=0)
+    return np.concatenate([one, two, one], axis=0)
 
 
 class Lift:
@@ -78,41 +77,25 @@
     lax.fori_loop(0, count, step, 0)
 
 
-def split_store(target, row, lane, value):
-    one = value.astype(BF16)
-    rest = value - one.astype(F32)
-    two = rest.astype(BF16)
-    three = (rest - two.astype(F32)).astype(BF16)
-    rows = pl.ds(row, 16)
-    target[0, rows, lane : lane + 128] = one
-    target[1, rows, lane : lane + 128] = two
-    target[2, rows, lane : lane + 128] = three
-
-
-def along_y(load, block, x_high, store):
+def along_y(load, x_high, wanted, put):
     lift = Lift(load)
-    half = block // 2
-    values = []
-    for i in range(half):
-        value = lift.low(i)
-        values.append(value if x_high else value * (scaling * scaling))
-    for i in range(half):
-        value = lift.high(i)
-        values.append(value * (1.0 / (scaling * scaling)) if x_high else value)
-    for n in range(0, block, 2):
-        store(n * 8, jnp.concatenate([values[n], values[n + 1]], axis=0))
-
-
-def along_z(split, table, row, rows):
-    at = pl.ds(row, rows)
-    one, two, three = split[0, at, :], split[1, at, :], split[2, at, :]
-    left = jnp.concatenate([one, one, two, two, one, three], axis=1)
+    for y_high, j in wanted:
+        value = lift.high(j) if y_high else lift.low(j)
+        if x_high == y_high:
+            value = value * (scaling**-2 if x_high else scaling**2)
+        put(y_high, j, value)
+
+
+def along_z(rows, table):
+    high = rows.astype(BF16)
+    rest = (rows - high.astype(F32)).astype(BF16)
+    left = jnp.concatenate([high, high, rest], axis=1)
     return jnp.dot(left, table[...], preferred_element_type=F32)
 
 
 def kernel(count_x, count_y, v, t1, t2, t3, d1, s1, d2, s2, d3, s3, coarse,
-           cells, bands, split, second, third, last, stage, w1, w2, w3,
-           cs1, cr1, cs2, cr2, cs3, cr3, bands_low, split_low, own_sem, send_sem, recv_sem):
+           cells, inner, outer, mixed, second, third, last, stage, w1, w2, w3,
+           cs1, cr1, cs2, cr2, cs3, cr3, bands_low, own_sem, send_sem, recv_sem):
     gx, gy = lax.axis_index("gx"), lax.axis_index("gy")
     right, left = lax.rem(gx + 1, count_x), lax.rem(gx + count_x - 1, count_x)
     up, down = lax.rem(gy + 1, count_y), lax.rem(gy + count_y - 1, count_y)
@@ -171,55 +154,69 @@
     for copy in y_halo:
         copy.wait_recv()
 
-    def level_one(g, lows, highs):
-        wanted = [(0, k) for k in lows] + [(1, k) for k in highs]
-
-        def field(t):
-            other = lax.rem(t + 3, 4)
-            index = 3 + lax.div((t + 1) * (6 - t), 2) + g - (6 - t)
-
-            def along_x(i):
-                rows = pl.ds(pl.multiple_of(i * 8, 8), 8)
-                for h in range(2):
-                    lanes = slice(128 * h, 128 * h + 128)
-                    lift = Lift(lambda n: cells[g, 4 + n, rows, lanes] * cells[other, 4 + n, rows, lanes])
-                    for n, (x_high, k) in enumerate(wanted):
-                        bands[n, h, rows, :] = lift.high(k) if x_high else lift.low(k)
-
-            loop(10, along_x)
-
-            def y_band(x_high):
-                def one(n):
-                    n = n + len(lows) if x_high else n
-                    for h in range(2):
-                        along_y(
-                            lambda r: bands[n, h, pl.ds(8 + r, 8, stride=8), :],
-                            8,
-                            x_high,
-                            lambda at, value: split_store(split, pl.multiple_of(n * 64 + at, 16), 128 * h, value),
-                        )
-
-                return one
-
-            loop(len(lows), y_band(0))
-            loop(len(highs), y_band(1))
-            for n, (x_high, k) in enumerate(wanted):
-                out = along_z(split, w1, n * 64, 64)
-                for y_high in range(2):
-                    for j in range(4):
-                        at = y_high * 32 + j * 8
-                        for z_high in range(2):
-                            value = out[at : at + 8, 128 * z_high : 128 * z_high + 128]
-                            band = 4 * z_high + 2 * y_high + x_high
-                            if band:
-                                d1[band - 1, index, k, pl.ds(j, 8, stride=4), :] = value
-                            else:
-                                second[index, k, pl.ds(8 + j, 8, stride=4), :] = value
-
-        loop(g + 2, field)
+    def index_of(g, t):
+        return 3 + lax.div((t + 1) * (6 - t), 2) + g - (6 - t)
+
+    def lift_x(g, t, wanted, put):
+        other = lax.rem(t + 3, 4)
+
+        def tile(i):
+            rows = pl.ds(pl.multiple_of(i * 8, 8), 8)
+            for h in range(2):
+                lanes = slice(128 * h, 128 * h + 128)
+                lift = Lift(lambda n: cells[g, 4 + n, rows, lanes] * cells[other, 4 + n, rows, lanes])
+                for n, (x_high, k) in enumerate(wanted):
+                    put(n, h, rows, lift.high(k) if x_high else lift.low(k))
+
+        loop(10, tile)
+
+    def lift_y(load, x_high, y_wanted, at):
+        for h in range(2):
+            for q in range(2):
+
+                def put(y_high, j, value):
+                    mixed[pl.ds(pl.multiple_of(at(y_high) + 16 * q + 8 * j, 8), 8), 128 * h : 128 * h + 128] = value
+
+                wanted = [(y_high, j) for y_high in y_wanted for j in range(2)]
+                along_y(lambda r: load(h, pl.ds(8 + 32 * q + r, 8, stride=4)), x_high, wanted, put)
+
+    def lift_z(pieces):
+        out = along_z(mixed[0 : 32 * len(pieces), :], w1)
+        for n, (index, x_high, k, y_high) in enumerate(pieces):
+            for q in range(2):
+                for j in range(2):
+                    at = 32 * n + 16 * q + 8 * j
+                    for z_high in range(2):
+                        value = out[at : at + 8, 128 * z_high : 128 * z_high + 128]
+                        band = 4 * z_high + 2 * y_high + x_high
+                        row = 16 * q + j
+                        if band:
+                            d1[band - 1, index, k, pl.ds(row, 8, stride=2), :] = value
+                        else:
+                            second[index, k, pl.ds(8 + row, 8, stride=2), :] = value
+
+    inner_wanted = [(0, k) for k in (2, 3, 4, 5)] + [(1, k) for k in (1, 2, 3, 4, 5)]
+    outer_wanted = [(0, k) for k in (0, 1, 6, 7)] + [(1, k) for k in (0, 6, 7)]
+
+    def inner_field(g, t):
+        def put(n, h, rows, value):
+            inner[n, h, rows, :] = value
+
+        lift_x(g, t, inner_wanted, put)
+
+        def low(n):
+            lift_y(lambda h, at: inner[n, h, at, :], 0, (0, 1), lambda y_high: n * 64 + 32 * y_high)
+
+        def high(n):
+            lift_y(lambda h, at: inner[4 + n, h, at, :], 1, (0, 1), lambda y_high: (4 + n) * 64 + 32 * y_high)
+
+        loop(4, low)
+        loop(5, high)
+        lift_z([(index_of(g, t), x_high, k, y_high) for x_high, k in inner_wanted for y_high in range(2)])
 
     for g in range(3):
-        level_one(g, (2, 3, 4, 5), (1, 2, 3, 4, 5))
+        loop(g + 2, lambda t: inner_field(g, t))
+
     for g in range(3):
         for copy in x_halo[g]:
             copy.wait_recv()
@@ -232,7 +229,34 @@
                         for u in range(2):
                             if layer + 2 * m + u < 23:
                                 cells[c, layer + 2 * m + u, row : row + 4, :] = cr1[k, c, m, 4 * u : 4 * u + 4, :]
-        level_one(g, (0, 1, 6, 7), (0, 6, 7))
+
+        def outer_field(t):
+            index = index_of(g, t)
+
+            def put(n, h, rows, value):
+                outer[index, n, h, rows, :] = value
+
+            lift_x(g, t, outer_wanted, put)
+
+            def low(n):
+                lift_y(lambda h, at: outer[index, n, h, at, :], 0, (0,), lambda y_high: t * 128 + n * 32)
+
+            loop(4, low)
+
+        loop(g + 2, outer_field)
+        lift_z([(3 + (t + 1) * (6 - t) // 2 + g - (6 - t), x_high, k, 0) for t in range(g + 2) for x_high, k in outer_wanted[:4]])
+
+    def outer_details(index):
+        def low(n):
+            lift_y(lambda h, at: outer[index, n, h, at, :], 0, (1,), lambda y_high: n * 32)
+
+        def high(n):
+            lift_y(lambda h, at: outer[index, 4 + n, h, at, :], 1, (0, 1), lambda y_high: 128 + n * 64 + 32 * y_high)
+
+        loop(4, low)
+        loop(3, high)
+        pieces = [(index, x_high, k, 1) for x_high, k in outer_wanted[:4]]
+        lift_z(pieces + [(index, x_high, k, y_high) for x_high, k in outer_wanted[4:] for y_high in range(2)])
 
     def exchange(field, n, rows, cs, cr):
         def prepare(f):
@@ -302,21 +326,23 @@
 
             loop(rows // 8 + 2, along_x)
 
+            wanted = [(y_high, j) for y_high in range(2) for j in range(block // 2)]
+
             def y_band(x_high):
                 def one(k):
                     k = k + half if x_high else k
-                    along_y(
-                        lambda r: bands_low[k, pl.ds(8 + r, 8, stride=block), :],
-                        block,
-                        x_high,
-                        lambda at, value: split_store(split_low, pl.multiple_of(k * rows + at, 16), 0, value),
-                    )
+
+                    def put_row(y_high, j, value):
+                        at = k * rows + y_high * (rows // 2) + j * 8
+                        mixed[pl.ds(pl.multiple_of(at, 8), 8), 0:128] = value
+
+                    along_y(lambda r: bands_low[k, pl.ds(8 + r, 8, stride=block), :], x_high, wanted, put_row)
 
                 return one
 
             loop(half, y_band(0))
             loop(half, y_band(1))
-            out = along_z(split_low, table, 0, n * rows)
+            out = along_z(mixed[0 : n * rows, 0:128], table)
             for k in range(n):
                 x_high, x_at = divmod(k, half)
                 for y_high in range(2):
@@ -330,6 +356,7 @@
 
     finish = exchange(second, 8, 32, cs2, cr2)
     stresses(s1, second, 8, slice(8, 40))
+    loop(9, outer_details)
     finish()
 
     def put_two(f, band, k, j, value):
@@ -359,25 +386,35 @@
         copy.wait_send()
 
 
+def flush(*refs):
+    copies = [pltpu.make_async_copy(refs[n], refs[7 + n], refs[14].at[n]) for n in range(7)]
+    for copy in copies:
+        copy.start()
+    for copy in copies:
+        copy.wait()
+
+
 def body(velocity):
     shapes = ((7, 9, 8, 32, 128), (6, 8, 32, 128), (7, 9, 4, 16, 64), (6, 4, 16, 64), (7, 9, 2, 8, 32), (6, 2, 8, 32), (3, 2, 8, 32))
     copies = 12 + 8 + 8
+    limit = 50_000_000
     run = pl.pallas_call(
         lambda *refs: kernel(lax.axis_size("gx"), lax.axis_size("gy"), *refs),
-        out_shape=[jax.ShapeDtypeStruct(shape, F32) for shape in shapes],
+        out_shape=[pltpu.VMEM(shape, F32) for shape in shapes],
         in_specs=[pl.BlockSpec(memory_space=pltpu.HBM)] * 4,
         out_specs=[pl.BlockSpec(memory_space=pltpu.VMEM)] * 7,
         scratch_shapes=[
             pltpu.VMEM((4, 23, 80, 256), F32),
             pltpu.VMEM((9, 2, 80, 128), F32),
-            pltpu.VMEM((3, 576, 256), BF16),
+            pltpu.VMEM((9, 7, 2, 80, 128), F32),
+            pltpu.VMEM((576, 256), F32),
             pltpu.VMEM((9, 16, 48, 128), F32),
             pltpu.VMEM((9, 12, 32, 128), F32),
             pltpu.VMEM((9, 2, 8, 128), F32),
             pltpu.VMEM((7, 4, 16, 128), F32),
-            pltpu.VMEM((1536, 256), BF16),
             pltpu.VMEM((768, 256), BF16),
-            pltpu.VMEM((768, 256), BF16),
+            pltpu.VMEM((384, 256), BF16),
+            pltpu.VMEM((384, 256), BF16),
             pltpu.VMEM((4, 3, 2, 8, 256), F32),
             pltpu.VMEM((4, 3, 2, 8, 256), F32),
             pltpu.VMEM((4, 9, 8, 128), F32),
@@ -385,14 +422,23 @@
             pltpu.VMEM((4, 9, 8, 128), F32),
             pltpu.VMEM((4, 9, 8, 128), F32),
             pltpu.VMEM((8, 48, 128), F32),
-            pltpu.VMEM((3, 256, 128), BF16),
             pltpu.SemaphoreType.DMA((6,)),
             pltpu.SemaphoreType.DMA((copies,)),
             pltpu.SemaphoreType.DMA((copies,)),
         ],
-        compiler_params=pltpu.CompilerParams(collective_id=0, has_side_effects=True, vmem_limit_bytes=34 << 20),
+        compiler_params=pltpu.CompilerParams(collective_id=0, has_side_effects=True, vmem_limit_bytes=limit),
     )
-    return tuple(run(velocity, third_table(256, 256), third_table(128, 128), third_table(64, 128)))
+    results = run(velocity, third_table(256, 256), third_table(128, 128), third_table(64, 128))
+    return tuple(
+        pl.pallas_call(
+            flush,
+            out_shape=[pltpu.HBM(shape, F32) for shape in shapes],
+            in_specs=[pl.BlockSpec(memory_space=pl.ANY)] * 7,
+            out_specs=[pl.BlockSpec(memory_space=pl.ANY)] * 7,
+            scratch_shapes=[pltpu.SemaphoreType.DMA((7,))],
+            compiler_params=pltpu.CompilerParams(vmem_limit_bytes=1_000_000),
+        )(*results)
+    )
 
 
 def solution(mesh):

time: 97.7 us -> 67.1 us (0.69)
  Pallas kernels: 83.6 us -> 66.4 us
  local copies, waits for them, and re-layouts: 13.2 us -> 0 us
    pallas_call x1, Pallas kernels: 83.6 us -> 61.9 us  [body(): run(velocity, third_table(256, 256), third_table(128, 128), third_table(6...]
    unnamed x15 -> x0, local copies, waits for them, and re-layouts: 13.2 us -> none
    pallas_call x0 -> x1, Pallas kernels: none -> 4.49 us  [body(): pl.pallas_call(flush, out_shape=[pltpu.HBM(shape, F32) for shape in shape...]
where the time goes in v1:
time: 67.1 us; the launch traced here: 67 us
  Pallas kernels  66.4 us (99%)
    pallas_call x1, Pallas kernels, body(): run(velocity, third_table(256, 256), third_table(128, 128), third_table(6...  61.9 us
    pallas_call x1, Pallas kernels, body(): pl.pallas_call(flush, out_shape=[pltpu.HBM(shape, F32) for shape in shape...  4.49 us

profile of v1, /device:TPU:1, one launch (start us, length us, event | category | flops | bytes accessed | tf_op | source)
XLA Modules:
  0.0 67.0 jit_solution(6348813955429788497)
XLA Ops:
  0.6 61.9 %shard_map.99 = (f32[7,9,8,32,128]{4,3,2,1,0:T(8,128)S(1)}, f32[6,8,32,128]{3,2,1,0:T(8,128)S(1)}, f32[7,9,4,16,64]{4,3,2,1,0:T(8,128)S(1)}, f32[6,4,16,64]{3,2,...) custom-call(f32[3,16,64,256]{3,2,1,0:T(8,128)} %refs_0_.1, ...), custom_call_target="tpu_custom_call" | custom-call | tf_op jit(solution)/shard_map/pallas_call | solution.py:431
  62.5 4.5 %shard_map.100 = (f32[7,9,8,32,128]{4,3,2,1,0:T(8,128)}, f32[6,8,32,128]{3,2,1,0:T(8,128)}, f32[7,9,4,16,64]{4,3,2,1,0:T(8,128)}, f32[6,4,16,64]{3,2,1,0:T(8,128...) custom-call(f32[7,9,8,32,128]{4,3,2,1,0:T(8,128)S(1)} %get-tuple-element.14.refs_0_, ...), custom_call_target="tpu_custom_call" | custom-call | tf_op jit(solution)/shard_map/pallas_call | solution.py:433

commit v2 on v1

v2 whole, which is shorter than its diff:
```python
import jax
import jax.numpy as jnp
import numpy as np
from jax import lax
from jax.experimental import pallas as pl
from jax.experimental.pallas import tpu as pltpu
from jax.sharding import PartitionSpec as P

MESH = pl.DeviceIdType.MESH
F32 = jnp.float32
BF16 = jnp.bfloat16

predict_one = -1.586134342
update_one = -0.05298011854
predict_two = 0.8829110762
update_two = 0.4435068522
scaling = 1.149604398
product_pairs = ((0, 0), (0, 1), (0, 2), (1, 1), (1, 2), (2, 2))


def three_products(table, axis):
    one = table.astype(np.float32).astype(BF16)
    two = (table - one.astype(np.float64)).astype(np.float32).astype(BF16)
    return np.concatenate([one, two, one] if axis == 0 else [one, one, two], axis=axis)


def lift_table(cells, ahead, behind):
    even, odd = cells[0::2], cells[1::2]
    odd = odd + predict_one * (even + ahead(even))
    even = even + update_one * (odd + behind(odd))
    odd = odd + predict_two * (even + ahead(even))
    even = even + update_two * (odd + behind(odd))
    return even, odd


def third_table(length, rows):
    even, odd = lift_table(
        np.eye(length), lambda v: np.concatenate([v[1:], v[-1:]]), lambda v: np.concatenate([v[:1], v[:-1]])
    )
    table = np.zeros((rows, 256))
    table[:length, : length // 2] = even.T * scaling
    table[:length, 128 : 128 + length // 2] = odd.T / scaling
    return three_products(table, 0)


def second_table(rows, depth):
    even, odd = lift_table(
        np.eye(rows + 16), lambda v: np.concatenate([v[1:], v[-1:]]), lambda v: np.concatenate([v[:1], v[:-1]])
    )
    low, high = even[4 : 4 + rows // 2], odd[4 : 4 + rows // 2]
    tables = []
    for low_scale, high_scale in ((scaling**2, 1.0), (1.0, scaling**-2)):
        parts = three_products(np.concatenate([low * low_scale, high * high_scale]), 1)
        tables.append(np.concatenate([parts, np.zeros((rows, depth - parts.shape[1]), BF16)], axis=1))
    return np.stack(tables)


class Lift:
    def __init__(self, cell):
        self.cell = cell
        self.known = {}

    def get(self, key, make):
        if key not in self.known:
            self.known[key] = make()
        return self.known[key]

    def even(self, i):
        return self.get(("e", i), lambda: self.cell(2 * i))

    def odd(self, i):
        return self.get(("o", i), lambda: self.cell(2 * i + 1))

    def odd_one(self, i):
        return self.get(("o1", i), lambda: self.odd(i) + predict_one * (self.even(i) + self.even(i + 1)))

    def even_one(self, i):
        return self.get(("e1", i), lambda: self.even(i) + update_one * (self.odd_one(i - 1) + self.odd_one(i)))

    def high(self, i):
        return self.get(("o2", i), lambda: self.odd_one(i) + predict_two * (self.even_one(i) + self.even_one(i + 1)))

    def low(self, i):
        return self.get(("e2", i), lambda: self.even_one(i) + update_two * (self.high(i - 1) + self.high(i)))


def loop(count, body):
    def step(i, carry):
        body(i)
        return carry

    lax.fori_loop(0, count, step, 0)


def along_y(table, rows):
    high = rows.astype(BF16)
    rest = (rows - high.astype(F32)).astype(BF16)
    pad = table.shape[1] - 3 * rows.shape[0]
    right = jnp.concatenate([high, rest, high] + ([high[:pad]] if pad else []), axis=0)
    return jnp.dot(table, right, preferred_element_type=F32)


def along_z(rows, table):
    high = rows.astype(BF16)
    rest = (rows - high.astype(F32)).astype(BF16)
    left = jnp.concatenate([high, high, rest], axis=1)
    return jnp.dot(left, table[...], preferred_element_type=F32)


def kernel(count_x, count_y, v, z1, z2, z3, y1, y2, y3, d1, s1, d2, s2, d3, s3, coarse,
           cells, inner, outer, mixed, second, third, last, wz1, wz2, wz3, wy1, wy2, wy3,
           cs1, cr1, cs2, cr2, cs3, cr3, bands, own_sem, send_sem, recv_sem):
    gx, gy = lax.axis_index("gx"), lax.axis_index("gy")
    right, left = lax.rem(gx + 1, count_x), lax.rem(gx + count_x - 1, count_x)
    up, down = lax.rem(gy + 1, count_y), lax.rem(gy + count_y - 1, count_y)
    corners = ((right, up), (right, down), (left, up), (left, down))
    around = ((right, gy), (left, gy), (gx, up), (gx, down)) + corners

    own = [pltpu.make_async_copy(v.at[c], cells.at[c, 4:20, 8:72, :], own_sem.at[c]) for c in range(3)]
    pairs = ((z1, wz1), (z2, wz2), (z3, wz3), (y1, wy1), (y2, wy2), (y3, wy3))
    tables = [pltpu.make_async_copy(src, dst, own_sem.at[3 + n]) for n, (src, dst) in enumerate(pairs)]
    barrier = pltpu.get_barrier_semaphore()
    for device in around:
        pl.semaphore_signal(barrier, inc=1, device_id=device, device_id_type=MESH)
    for copy in own + tables:
        copy.start()
    pl.semaphore_wait(barrier, 8)

    started = []

    def send(src, dst, device):
        n = len(started)
        copy = pltpu.make_async_remote_copy(
            src_ref=src, dst_ref=dst, send_sem=send_sem.at[n], recv_sem=recv_sem.at[n], device_id=device, device_id_type=MESH
        )
        copy.start()
        started.append(copy)
        return copy

    def send_x(c):
        return (
            send(v.at[c, 12:16], cells.at[c, 0:4, 8:72, :], (right, gy)),
            send(v.at[c, 0:3], cells.at[c, 20:23, 8:72, :], (left, gy)),
        )

    def index_of(g, t):
        return 3 + ((t + 1) * (6 - t)) // 2 + g - (6 - t)

    slots = {index_of(g, t): (0, 2, 5)[g] + t for g in range(3) for t in range(g + 2)}

    x_halo = [send_x(0)]
    y_halo = (
        send(v.at[:, :, 56:64, :], cells.at[0:3, 4:20, 0:8, :], (gx, up)),
        send(v.at[:, :, 0:8, :], cells.at[0:3, 4:20, 72:80, :], (gx, down)),
    )
    for copy in own:
        copy.wait()
    for k, (layer, row) in enumerate(((16, 68), (16, 8), (4, 68), (4, 8))):
        for c in range(3):
            for m in range(2):
                for u in range(2):
                    cs1[k, c, m, 4 * u : 4 * u + 4, :] = cells[c, layer + 2 * m + u, row : row + 4, :]

    def fill(i):
        cells[3, i] = jnp.ones((80, 256), F32)

    loop(23, fill)
    corner_halo = [send(cs1.at[k], cr1.at[k], corners[k]) for k in range(4)]
    x_halo += [send_x(1), send_x(2)]
    for row in (0, 72):
        for layer in (0, 1, 2, 3, 20, 21, 22):
            for c in range(3):
                cells[c, layer, row : row + 8, :] = jnp.zeros((8, 256), F32)
    for f in range(9):
        for layer in range(8, 12):
            for row in (0, 40):
                second[f, layer, row : row + 8, :] = jnp.zeros((8, 128), F32)
        for layer in range(4, 6):
            for row in (0, 24):
                third[f, layer, row : row + 8, :] = jnp.zeros((8, 128), F32)
    for copy in tables:
        copy.wait()
    for copy in y_halo:
        copy.wait_recv()

    def lift_x(g, t, wanted, put):
        other = lax.rem(t + 3, 4)

        def tile(i):
            rows = pl.ds(pl.multiple_of(i * 8, 8), 8)
            for h in range(2):
                lanes = slice(128 * h, 128 * h + 128)
                lift = Lift(lambda n: cells[g, 4 + n, rows, lanes] * cells[other, 4 + n, rows, lanes])
                for n, (x_high, k) in enumerate(wanted):
                    put(n, rows, lanes, lift.high(k) if x_high else lift.low(k))

        loop(10, tile)

    def lift_z(pieces):
        out = along_z(mixed[0 : 32 * len(pieces), :], wz1)
        for n, (index, slot, x_high, k, y_high) in enumerate(pieces):
            for z_high in range(2):
                value = out[32 * n : 32 * n + 32, 128 * z_high : 128 * z_high + 128]
                band = 4 * z_high + 2 * y_high + x_high
                if band:
                    d1[band - 1, index, k] = value
                else:
                    second[slot, k, 8:40, :] = value

    inner_wanted = [(0, k) for k in (2, 3, 4, 5)] + [(1, k) for k in (1, 2, 3, 4, 5)]
    outer_wanted = [(0, k) for k in (0, 1, 6, 7)] + [(1, k) for k in (0, 6, 7)]

    def inner_field(g, t):
        index = 3 + lax.div((t + 1) * (6 - t), 2) + g - (6 - t)

        def put(n, rows, lanes, value):
            inner[n, rows, lanes] = value

        lift_x(g, t, inner_wanted, put)
        for n, (x_high, k) in enumerate(inner_wanted):
            mixed[n * 64 : n * 64 + 64, :] = along_y(wy1[x_high], inner[n])
        lift_z([(index, (0, 2, 5)[g] + t, x_high, k, y_high) for x_high, k in inner_wanted for y_high in range(2)])

    def outer_group(g):
        for copy in x_halo[g]:
            copy.wait_recv()
        if g == 0:
            for copy in corner_halo:
                copy.wait_recv()
            for k, (layer, row) in enumerate(((0, 4), (0, 72), (20, 4), (20, 72))):
                for c in range(3):
                    for m in range(2):
                        for u in range(2):
                            if layer + 2 * m + u < 23:
                                cells[c, layer + 2 * m + u, row : row + 4, :] = cr1[k, c, m, 4 * u : 4 * u + 4, :]
        base = (0, 2, 5)[g]

        def outer_field(t):
            slot = base + t

            def put(n, rows, lanes, value):
                outer[slot, n, rows, lanes] = value

            lift_x(g, t, outer_wanted, put)
            for n in range(4):
                at = pl.ds(pl.multiple_of(t * 128 + n * 32, 32), 32)
                mixed[at, :] = along_y(wy1[0, 0:32], outer[slot, n])

        loop(g + 2, outer_field)
        lift_z([(index_of(g, t), base + t, x_high, k, 0) for t in range(g + 2) for x_high, k in outer_wanted[:4]])

    def outer_details(g):
        def one(t):
            index = 3 + lax.div((t + 1) * (6 - t), 2) + g - (6 - t)
            slot = (0, 2, 5)[g] + t
            for n in range(4):
                mixed[n * 32 : n * 32 + 32, :] = along_y(wy1[0, 32:64], outer[slot, n])
            for n in range(3):
                mixed[128 + n * 64 : 192 + n * 64, :] = along_y(wy1[1], outer[slot, 4 + n])
            pieces = [(index, slot, x_high, k, 1) for x_high, k in outer_wanted[:4]]
            lift_z(pieces + [(index, slot, x_high, k, y_high) for x_high, k in outer_wanted[4:] for y_high in range(2)])

        loop(g + 2, one)

    def exchange_two(g):
        n, rows, field = 8, 32, second
        at_group = pl.ds((0, 2, 5)[g], g + 2)

        def prepare(t):
            f = (0, 2, 5)[g] + t
            for i in range(rows // 8):
                at = pl.ds(8 + i * 8, 8)
                layer = lambda l: field[f, l, at, :]
                field[f, n + 4, at, :] = layer(n - 1) + predict_one * layer(n - 2)
                before = layer(n - 3) + predict_one * (layer(n - 4) + layer(n - 2))
                field[f, n + 5, at, :] = layer(n - 2) + update_one * before
                field[f, n + 6, at, :] = layer(0)
                field[f, n + 7, at, :] = layer(1) + predict_one * (layer(0) + layer(2))
            for k, (layer, row) in enumerate(((n + 4, 4 + rows), (n + 4, 8), (n + 6, 4 + rows), (n + 6, 8))):
                for u in range(2):
                    cs2[k, f, 4 * u : 4 * u + 4, :] = field[f, layer + u, row : row + 4, :]

        loop(g + 2, prepare)
        whole = slice(8, 8 + rows)
        halo = [
            send(field.at[at_group, n + 4 : n + 6, whole, :], field.at[at_group, n : n + 2, whole, :], (right, gy)),
            send(field.at[at_group, n + 6 : n + 8, whole, :], field.at[at_group, n + 2 : n + 4, whole, :], (left, gy)),
        ]
        halo += [send(cs2.at[k, at_group], cr2.at[k, at_group], corners[k]) for k in range(4)]
        halo += [
            send(field.at[at_group, 0:n, rows : rows + 8, :], field.at[at_group, 0:n, 0:8, :], (gx, up)),
            send(field.at[at_group, 0:n, 8:16, :], field.at[at_group, 0:n, 8 + rows : 16 + rows, :], (gx, down)),
        ]

        def finish():
            for copy in halo:
                copy.wait_recv()
            for t in range(g + 2):
                f = (0, 2, 5)[g] + t
                for k, (layer, row) in enumerate(((n, 4), (n, 8 + rows), (n + 2, 4), (n + 2, 8 + rows))):
                    for u in range(2):
                        field[f, layer + u, row : row + 4, :] = cr2[k, f, 4 * u : 4 * u + 4, :]

        return finish

    def exchange_three(g):
        n, rows, field = 4, 16, third
        at_group = pl.ds((0, 2, 5)[g], g + 2)
        at_pairs = pl.ds((0, 1, 3)[g], (1, 2, 2)[g])
        for t in range(g + 2):
            f = (0, 2, 5)[g] + t
            for i in range(rows // 8):
                at = pl.ds(8 + i * 8, 8)
                layer = lambda l: field[f, l, at, :]
                before = layer(1) + predict_one * (layer(0) + layer(2))
                p, q = layer(3) + predict_one * layer(2), layer(2) + update_one * before
                field[f, 6, at, :] = p + pltpu.roll(q, 64, 1)
                field[f, 7, at, :] = layer(0) + pltpu.roll(before, 64, 1)
            pair, half = (0, 1, 3)[g] + t // 2, 4 * (t % 2)
            for k, (layer, row) in enumerate(((6, 4 + rows), (6, 8), (7, 4 + rows), (7, 8))):
                cs3[k, pair, half : half + 4, :] = field[f, layer, row : row + 4, :]
        whole = slice(8, 8 + rows)
        halo = [
            send(field.at[at_group, 6:7, whole, :], field.at[at_group, 4:5, whole, :], (right, gy)),
            send(field.at[at_group, 7:8, whole, :], field.at[at_group, 5:6, whole, :], (left, gy)),
        ]
        halo += [send(cs3.at[k, at_pairs], cr3.at[k, at_pairs], corners[k]) for k in range(4)]
        halo += [
            send(field.at[at_group, 0:n, rows : rows + 8, :], field.at[at_group, 0:n, 0:8, :], (gx, up)),
            send(field.at[at_group, 0:n, 8:16, :], field.at[at_group, 0:n, 8 + rows : 16 + rows, :], (gx, down)),
        ]

        def finish():
            for copy in halo:
                copy.wait_recv()
            for t in range(g + 2):
                f, pair, half = (0, 2, 5)[g] + t, (0, 1, 3)[g] + t // 2, 4 * (t % 2)
                for k, (layer, row) in enumerate(((4, 4), (4, 8 + rows), (5, 4), (5, 8 + rows))):
                    field[f, layer, row : row + 4, :] = cr3[k, pair, half : half + 4, :]

        return finish

    def stresses(target, field, n, at):
        def layer(l):
            for k, (p, q) in enumerate(product_pairs):
                value = field[slots[3 + k], l, at, :] - field[slots[p], l, at, :] * field[slots[q], l, at, :]
                target[k, l] = value[:, : target.shape[3]]

        loop(n, layer)

    def level(g, field, n, rows, halo_of, wy, wz, put):
        half = n // 2

        def one_field(t):
            slot = (0, 2, 5)[g] + t
            index = 3 + lax.div((t + 1) * (6 - t), 2) + g - (6 - t)

            def along_x(i):
                at = pl.ds(pl.multiple_of(i * 8, 8), 8)
                p, q, next_even, next_odd = halo_of(slot, at)
                lift = Lift(lambda l: field[slot, l, at, :] if l < n else next_even)
                lift.known[("o1", -1)] = p + predict_one * lift.even(0)
                lift.known[("e1", -1)] = q + update_one * lift.odd_one(-1)
                lift.known[("o1", half)] = next_odd
                for k in range(half):
                    bands[k, at, :] = lift.low(k)
                    bands[half + k, at, :] = lift.high(k)

            loop(rows // 8 + 2, along_x)
            whole = rows + 16
            for k in range(0, n, 2):
                two = jnp.concatenate([bands[k, 0:whole, :], bands[k + 1, 0:whole, :]], axis=1)
                out = along_y(wy[k // half], two)
                mixed[k * rows : k * rows + rows, 0:128] = out[:, :128]
                mixed[k * rows + rows : k * rows + 2 * rows, 0:128] = out[:, 128:]
            out = along_z(mixed[0 : n * rows, 0:128], wz)
            for k in range(n):
                x_high, x_at = divmod(k, half)
                for y_high in range(2):
                    at = k * rows + y_high * (rows // 2)
                    for z_high in range(2):
                        value = out[at : at + rows // 2, 128 * z_high : 128 * z_high + 128]
                        put(index, slot, 4 * z_high + 2 * y_high + x_high, x_at, value)

        loop(g + 2, one_field)

    def halo_two(slot, at):
        return tuple(second[slot, 8 + l, at, :] for l in range(4))

    def put_two(index, slot, band, k, value):
        if band:
            d2[band - 1, index, k] = value[:, :64]
        else:
            third[slot, k, 8:24, :] = value

    def halo_three(slot, at):
        before, after = third[slot, 4, at, :], third[slot, 5, at, :]
        return before, pltpu.roll(before, 64, 1), after, pltpu.roll(after, 64, 1)

    def put_three(index, slot, band, k, value):
        if band:
            d3[band - 1, index, k] = value[:, :32]
        else:
            last[slot, k] = value

    for g in range(3):
        loop(g + 2, lambda t: inner_field(g, t))
    finish_two = []
    for g in range(3):
        outer_group(g)
        finish_two.append(exchange_two(g))
    for g in range(3):
        outer_details(g)
    stresses(s1, second, 8, slice(8, 40))
    finish_three = []
    for g in range(3):
        finish_two[g]()
        level(g, second, 8, 32, halo_two, wy2, wz2, put_two)
        finish_three.append(exchange_three(g))
    stresses(s2, third, 4, slice(8, 24))
    for g in range(3):
        finish_three[g]()
        level(g, third, 4, 16, halo_three, wy3, wz3, put_three)
    stresses(s3, last, 2, slice(0, 8))
    for c in range(3):
        coarse[c] = last[slots[c]][:, :, :32]
    for copy in started:
        copy.wait_send()


def flush(*refs):
    copies = [pltpu.make_async_copy(refs[n], refs[7 + n], refs[14].at[n]) for n in range(7)]
    for copy in copies:
        copy.start()
    for copy in copies:
        copy.wait()


def body(velocity):
    shapes = ((7, 9, 8, 32, 128), (6, 8, 32, 128), (7, 9, 4, 16, 64), (6, 4, 16, 64), (7, 9, 2, 8, 32), (6, 2, 8, 32), (3, 2, 8, 32))
    copies = 12 + 24 + 24
    limit = 50_000_000
    run = pl.pallas_call(
        lambda *refs: kernel(lax.axis_size("gx"), lax.axis_size("gy"), *refs),
        out_shape=[pltpu.VMEM(shape, F32) for shape in shapes],
        in_specs=[pl.BlockSpec(memory_space=pltpu.HBM)] * 7,
        out_specs=[pl.BlockSpec(memory_space=pltpu.VMEM)] * 7,
        scratch_shapes=[
            pltpu.VMEM((4, 23, 80, 256), F32),
            pltpu.VMEM((9, 80, 256), F32),
            pltpu.VMEM((9, 7, 80, 256), F32),
            pltpu.VMEM((576, 256), F32),
            pltpu.VMEM((9, 16, 48, 128), F32),
            pltpu.VMEM((9, 8, 32, 128), F32),
            pltpu.VMEM((9, 2, 8, 128), F32),
            pltpu.VMEM((768, 256), BF16),
            pltpu.VMEM((384, 256), BF16),
            pltpu.VMEM((384, 256), BF16),
            pltpu.VMEM((2, 64, 256), BF16),
            pltpu.VMEM((2, 32, 144), BF16),
            pltpu.VMEM((2, 16, 96), BF16),
            pltpu.VMEM((4, 3, 2, 8, 256), F32),
            pltpu.VMEM((4, 3, 2, 8, 256), F32),
            pltpu.VMEM((4, 9, 8, 128), F32),
            pltpu.VMEM((4, 9, 8, 128), F32),
            pltpu.VMEM((4, 5, 8, 128), F32),
            pltpu.VMEM((4, 5, 8, 128), F32),
            pltpu.VMEM((8, 48, 128), F32),
            pltpu.SemaphoreType.DMA((9,)),
            pltpu.SemaphoreType.DMA((copies,)),
            pltpu.SemaphoreType.DMA((copies,)),
        ],
        compiler_params=pltpu.CompilerParams(collective_id=0, has_side_effects=True, vmem_limit_bytes=limit),
    )
    along_third = (third_table(256, 256), third_table(128, 128), third_table(64, 128))
    along_second = (second_table(64, 256), second_table(32, 144), second_table(16, 96))
    results = run(velocity, *along_third, *along_second)
    return tuple(
        pl.pallas_call(
            flush,
            out_shape=[pltpu.HBM(shape, F32) for shape in shapes],
            in_specs=[pl.BlockSpec(memory_space=pl.ANY)] * 7,
            out_specs=[pl.BlockSpec(memory_space=pl.ANY)] * 7,
            scratch_shapes=[pltpu.SemaphoreType.DMA((7,))],
            compiler_params=pltpu.CompilerParams(vmem_limit_bytes=1_000_000),
        )(*results)
    )


def solution(mesh):
    in_specs = (P(None, "gx", "gy", None),)
    out_specs = (
        P(None, None, "gx", "gy", None),
        P(None, "gx", "gy", None),
        P(None, None, "gx", "gy", None),
        P(None, "gx", "gy", None),
        P(None, None, "gx", "gy", None),
        P(None, "gx", "gy", None),
        P(None, "gx", "gy", None),
    )
    return jax.shard_map(body, mesh=mesh, in_specs=in_specs, out_specs=out_specs, check_vma=False)
```

time: 67.1 us -> 56.3 us (0.84)
  Pallas kernels: 66.4 us -> 55.5 us
    pallas_call x1, Pallas kernels: 61.9 us -> 51 us  [body(): results = run(velocity, *along_third, *along_second)]
where the time goes in v2:
time: 56.3 us; the launch traced here: 56.2 us
  Pallas kernels  55.5 us (99%)
  between operations  0.64 us (1%)
    pallas_call x1, Pallas kernels, body(): results = run(velocity, *along_third, *along_second)  51 us
    pallas_call x1, Pallas kernels, body(): pl.pallas_call(flush, out_shape=[pltpu.HBM(shape, F32) for shape in shape...  4.49 us

profile of v2, /device:TPU:1, one launch (start us, length us, event | category | flops | bytes accessed | tf_op | source)
XLA Modules:
  0.0 56.2 jit_solution(13313723760339173448)
XLA Ops:
  0.6 51.0 %shard_map.126 = (f32[7,9,8,32,128]{4,3,2,1,0:T(8,128)S(1)}, f32[6,8,32,128]{3,2,1,0:T(8,128)S(1)}, f32[7,9,4,16,64]{4,3,2,1,0:T(8,128)S(1)}, f32[6,4,16,64]{3,2...) custom-call(f32[3,16,64,256]{3,2,1,0:T(8,128)} %refs_0_.1, ...), custom_call_target="tpu_custom_call" | custom-call | tf_op jit(solution)/shard_map/pallas_call | solution.py:477
  51.7 4.5 %shard_map.127 = (f32[7,9,8,32,128]{4,3,2,1,0:T(8,128)}, f32[6,8,32,128]{3,2,1,0:T(8,128)}, f32[7,9,4,16,64]{4,3,2,1,0:T(8,128)}, f32[6,4,16,64]{3,2,1,0:T(8,128...) custom-call(f32[7,9,8,32,128]{4,3,2,1,0:T(8,128)S(1)} %get-tuple-element.14.refs_0_, ...), custom_call_target="tpu_custom_call" | custom-call | tf_op jit(solution)/shard_map/pallas_call | solution.py:479

commit v3 on v2

--- a/solution.py
+++ b/solution.py
@@ -149,10 +149,13 @@
     slots = {index_of(g, t): (0, 2, 5)[g] + t for g in range(3) for t in range(g + 2)}
 
     x_halo = [send_x(0)]
-    y_halo = (
-        send(v.at[:, :, 56:64, :], cells.at[0:3, 4:20, 0:8, :], (gx, up)),
-        send(v.at[:, :, 0:8, :], cells.at[0:3, 4:20, 72:80, :], (gx, down)),
-    )
+    y_halo = [
+        (
+            send(v.at[c, :, 56:64, :], cells.at[c, 4:20, 0:8, :], (gx, up)),
+            send(v.at[c, :, 0:8, :], cells.at[c, 4:20, 72:80, :], (gx, down)),
+        )
+        for c in range(3)
+    ]
     for copy in own:
         copy.wait()
     for k, (layer, row) in enumerate(((16, 68), (16, 8), (4, 68), (4, 8))):
@@ -180,8 +183,6 @@
                 third[f, layer, row : row + 8, :] = jnp.zeros((8, 128), F32)
     for copy in tables:
         copy.wait()
-    for copy in y_halo:
-        copy.wait_recv()
 
     def lift_x(g, t, wanted, put):
         other = lax.rem(t + 3, 4)
@@ -221,87 +222,101 @@
             mixed[n * 64 : n * 64 + 64, :] = along_y(wy1[x_high], inner[n])
         lift_z([(index, (0, 2, 5)[g] + t, x_high, k, y_high) for x_high, k in inner_wanted for y_high in range(2)])
 
-    def outer_group(g):
-        for copy in x_halo[g]:
-            copy.wait_recv()
-        if g == 0:
-            for copy in corner_halo:
-                copy.wait_recv()
-            for k, (layer, row) in enumerate(((0, 4), (0, 72), (20, 4), (20, 72))):
-                for c in range(3):
-                    for m in range(2):
-                        for u in range(2):
-                            if layer + 2 * m + u < 23:
-                                cells[c, layer + 2 * m + u, row : row + 4, :] = cr1[k, c, m, 4 * u : 4 * u + 4, :]
+    sides = {"right": ((6, 7), (6, 7), 2, 5), "left": ((0, 1), (0,), 0, 4), "both": ((0, 1, 6, 7), (0, 6, 7), 0, 4)}
+
+    def unpack_corners(which):
+        for k in which:
+            corner_halo[k].wait_recv()
+            layer, row = ((0, 4), (0, 72), (20, 4), (20, 72))[k]
+            for c in range(3):
+                for m in range(2):
+                    for u in range(2):
+                        if layer + 2 * m + u < 23:
+                            cells[c, layer + 2 * m + u, row : row + 4, :] = cr1[k, c, m, 4 * u : 4 * u + 4, :]
+
+    def outer_group(g, side):
+        lows, highs, low_at, high_at = sides[side]
+        wanted = [(0, k) for k in lows] + [(1, k) for k in highs]
+        places = [low_at + n for n in range(len(lows))] + [high_at + n for n in range(len(highs))]
         base = (0, 2, 5)[g]
 
         def outer_field(t):
             slot = base + t
 
             def put(n, rows, lanes, value):
-                outer[slot, n, rows, lanes] = value
-
-            lift_x(g, t, outer_wanted, put)
-            for n in range(4):
-                at = pl.ds(pl.multiple_of(t * 128 + n * 32, 32), 32)
-                mixed[at, :] = along_y(wy1[0, 0:32], outer[slot, n])
+                outer[slot, places[n], rows, lanes] = value
+
+            lift_x(g, t, wanted, put)
+            for n in range(len(lows)):
+                at = pl.ds(pl.multiple_of(t * 32 * len(lows) + n * 32, 32), 32)
+                mixed[at, :] = along_y(wy1[0, 0:32], outer[slot, low_at + n])
 
         loop(g + 2, outer_field)
-        lift_z([(index_of(g, t), base + t, x_high, k, 0) for t in range(g + 2) for x_high, k in outer_wanted[:4]])
-
-    def outer_details(g):
+        lift_z([(index_of(g, t), base + t, 0, k, 0) for t in range(g + 2) for k in lows])
+
+    def outer_details(g, side):
+        lows, highs, low_at, high_at = sides[side]
+
         def one(t):
             index = 3 + lax.div((t + 1) * (6 - t), 2) + g - (6 - t)
             slot = (0, 2, 5)[g] + t
-            for n in range(4):
-                mixed[n * 32 : n * 32 + 32, :] = along_y(wy1[0, 32:64], outer[slot, n])
-            for n in range(3):
-                mixed[128 + n * 64 : 192 + n * 64, :] = along_y(wy1[1], outer[slot, 4 + n])
-            pieces = [(index, slot, x_high, k, 1) for x_high, k in outer_wanted[:4]]
-            lift_z(pieces + [(index, slot, x_high, k, y_high) for x_high, k in outer_wanted[4:] for y_high in range(2)])
+            for n in range(len(lows)):
+                mixed[n * 32 : n * 32 + 32, :] = along_y(wy1[0, 32:64], outer[slot, low_at + n])
+            for n in range(len(highs)):
+                at = 32 * len(lows) + n * 64
+                mixed[at : at + 64, :] = along_y(wy1[1], outer[slot, high_at + n])
+            pieces = [(index, slot, 0, k, 1) for k in lows]
+            lift_z(pieces + [(index, slot, 1, k, y_high) for k in highs for y_high in range(2)])
 
         loop(g + 2, one)
 
-    def exchange_two(g):
+    halo_of_two = {0: [], 1: [], 2: []}
+
+    def send_two(g, side):
         n, rows, field = 8, 32, second
-        at_group = pl.ds((0, 2, 5)[g], g + 2)
+        base = (0, 2, 5)[g]
+        at_group = pl.ds(base, g + 2)
+        start = n + 4 if side == "right" else n + 6
 
         def prepare(t):
-            f = (0, 2, 5)[g] + t
+            f = base + t
             for i in range(rows // 8):
                 at = pl.ds(8 + i * 8, 8)
                 layer = lambda l: field[f, l, at, :]
-                field[f, n + 4, at, :] = layer(n - 1) + predict_one * layer(n - 2)
-                before = layer(n - 3) + predict_one * (layer(n - 4) + layer(n - 2))
-                field[f, n + 5, at, :] = layer(n - 2) + update_one * before
-                field[f, n + 6, at, :] = layer(0)
-                field[f, n + 7, at, :] = layer(1) + predict_one * (layer(0) + layer(2))
-            for k, (layer, row) in enumerate(((n + 4, 4 + rows), (n + 4, 8), (n + 6, 4 + rows), (n + 6, 8))):
+                if side == "right":
+                    field[f, start, at, :] = layer(n - 1) + predict_one * layer(n - 2)
+                    before = layer(n - 3) + predict_one * (layer(n - 4) + layer(n - 2))
+                    field[f, start + 1, at, :] = layer(n - 2) + update_one * before
+                else:
+                    field[f, start, at, :] = layer(0)
+                    field[f, start + 1, at, :] = layer(1) + predict_one * (layer(0) + layer(2))
+            for k, row in enumerate((4 + rows, 8)):
+                k = k if side == "right" else k + 2
                 for u in range(2):
-                    cs2[k, f, 4 * u : 4 * u + 4, :] = field[f, layer + u, row : row + 4, :]
+                    cs2[k, f, 4 * u : 4 * u + 4, :] = field[f, start + u, row : row + 4, :]
 
         loop(g + 2, prepare)
         whole = slice(8, 8 + rows)
-        halo = [
-            send(field.at[at_group, n + 4 : n + 6, whole, :], field.at[at_group, n : n + 2, whole, :], (right, gy)),
-            send(field.at[at_group, n + 6 : n + 8, whole, :], field.at[at_group, n + 2 : n + 4, whole, :], (left, gy)),
-        ]
-        halo += [send(cs2.at[k, at_group], cr2.at[k, at_group], corners[k]) for k in range(4)]
-        halo += [
-            send(field.at[at_group, 0:n, rows : rows + 8, :], field.at[at_group, 0:n, 0:8, :], (gx, up)),
-            send(field.at[at_group, 0:n, 8:16, :], field.at[at_group, 0:n, 8 + rows : 16 + rows, :], (gx, down)),
-        ]
-
-        def finish():
-            for copy in halo:
-                copy.wait_recv()
-            for t in range(g + 2):
-                f = (0, 2, 5)[g] + t
-                for k, (layer, row) in enumerate(((n, 4), (n, 8 + rows), (n + 2, 4), (n + 2, 8 + rows))):
-                    for u in range(2):
-                        field[f, layer + u, row : row + 4, :] = cr2[k, f, 4 * u : 4 * u + 4, :]
-
-        return finish
+        to = start - 4
+        device, first = ((right, gy), 0) if side == "right" else ((left, gy), 2)
+        halo = [send(field.at[at_group, start : start + 2, whole, :], field.at[at_group, to : to + 2, whole, :], device)]
+        halo += [send(cs2.at[k, at_group], cr2.at[k, at_group], corners[k]) for k in (first, first + 1)]
+        if side == "left":
+            halo += [
+                send(field.at[at_group, 0:n, rows : rows + 8, :], field.at[at_group, 0:n, 0:8, :], (gx, up)),
+                send(field.at[at_group, 0:n, 8:16, :], field.at[at_group, 0:n, 8 + rows : 16 + rows, :], (gx, down)),
+            ]
+        halo_of_two[g].extend(halo)
+
+    def finish_two(g):
+        n, rows, field = 8, 32, second
+        for copy in halo_of_two[g]:
+            copy.wait_recv()
+        for t in range(g + 2):
+            f = (0, 2, 5)[g] + t
+            for k, (layer, row) in enumerate(((n, 4), (n, 8 + rows), (n + 2, 4), (n + 2, 8 + rows))):
+                for u in range(2):
+                    field[f, layer + u, row : row + 4, :] = cr2[k, f, 4 * u : 4 * u + 4, :]
 
     def exchange_three(g):
         n, rows, field = 4, 16, third
@@ -404,17 +419,27 @@
             last[slot, k] = value
 
     for g in range(3):
+        for copy in y_halo[g]:
+            copy.wait_recv()
         loop(g + 2, lambda t: inner_field(g, t))
-    finish_two = []
+    for g in range(2):
+        for copy in x_halo[g]:
+            copy.wait_recv()
+        if g == 0:
+            unpack_corners(range(4))
+        outer_group(g, "both")
+        send_two(g, "right")
+        send_two(g, "left")
+    for side, which in (("right", 1), ("left", 0)):
+        x_halo[2][which].wait_recv()
+        outer_group(2, side)
+        send_two(2, side)
     for g in range(3):
-        outer_group(g)
-        finish_two.append(exchange_two(g))
-    for g in range(3):
-        outer_details(g)
+        outer_details(g, "both")
     stresses(s1, second, 8, slice(8, 40))
     finish_three = []
     for g in range(3):
-        finish_two[g]()
+        finish_two(g)
         level(g, second, 8, 32, halo_two, wy2, wz2, put_two)
         finish_three.append(exchange_three(g))
     stresses(s2, third, 4, slice(8, 24))
@@ -429,7 +454,9 @@
 
 
 def flush(*refs):
-    copies = [pltpu.make_async_copy(refs[n], refs[7 + n], refs[14].at[n]) for n in range(7)]
+    sem = refs[14]
+    copies = [pltpu.make_async_copy(refs[n].at[k], refs[7 + n].at[k], sem.at[n, k]) for n in (0, 2) for k in range(7)]
+    copies += [pltpu.make_async_copy(refs[n], refs[7 + n], sem.at[n, 0]) for n in (1, 3, 4, 5, 6)]
     for copy in copies:
         copy.start()
     for copy in copies:
@@ -438,7 +465,7 @@
 
 def body(velocity):
     shapes = ((7, 9, 8, 32, 128), (6, 8, 32, 128), (7, 9, 4, 16, 64), (6, 4, 16, 64), (7, 9, 2, 8, 32), (6, 2, 8, 32), (3, 2, 8, 32))
-    copies = 12 + 24 + 24
+    copies = 16 + 24 + 24
     limit = 50_000_000
     run = pl.pallas_call(
         lambda *refs: kernel(lax.axis_size("gx"), lax.axis_size("gy"), *refs),
@@ -481,7 +508,7 @@
             out_shape=[pltpu.HBM(shape, F32) for shape in shapes],
             in_specs=[pl.BlockSpec(memory_space=pl.ANY)] * 7,
             out_specs=[pl.BlockSpec(memory_space=pl.ANY)] * 7,
-            scratch_shapes=[pltpu.SemaphoreType.DMA((7,))],
+            scratch_shapes=[pltpu.SemaphoreType.DMA((7, 7))],
             compiler_params=pltpu.CompilerParams(vmem_limit_bytes=1_000_000),
         )(*results)
     )

time: 56.3 us -> 55.8 us (level)
    pallas_call x1, Pallas kernels: 51 us -> 50.3 us  [body(): results = run(velocity, *along_third, *along_second)]
where the time goes in v3:
time: 55.8 us; the launch traced here: 55.7 us
  Pallas kernels  55.1 us (99%)
  between operations  0.64 us (1%)
    pallas_call x1, Pallas kernels, body(): results = run(velocity, *along_third, *along_second)  50.3 us
    pallas_call x1, Pallas kernels, body(): pl.pallas_call(flush, out_shape=[pltpu.HBM(shape, F32) for shape in shape...  4.76 us

profile of v3, /device:TPU:1, one launch (start us, length us, event | category | flops | bytes accessed | tf_op | source)
XLA Modules:
  0.0 55.7 jit_solution(9995618541342340952)
XLA Ops:
  0.6 50.3 %shard_map.126 = (f32[7,9,8,32,128]{4,3,2,1,0:T(8,128)S(1)}, f32[6,8,32,128]{3,2,1,0:T(8,128)S(1)}, f32[7,9,4,16,64]{4,3,2,1,0:T(8,128)S(1)}, f32[6,4,16,64]{3,2...) custom-call(f32[3,16,64,256]{3,2,1,0:T(8,128)} %refs_0_.1, ...), custom_call_target="tpu_custom_call" | custom-call | tf_op jit(solution)/shard_map/pallas_call | solution.py:504
  51.0 4.8 %shard_map.127 = (f32[7,9,8,32,128]{4,3,2,1,0:T(8,128)}, f32[6,8,32,128]{3,2,1,0:T(8,128)}, f32[7,9,4,16,64]{4,3,2,1,0:T(8,128)}, f32[6,4,16,64]{3,2,1,0:T(8,128...) custom-call(f32[7,9,8,32,128]{4,3,2,1,0:T(8,128)S(1)} %get-tuple-element.14.refs_0_, ...), custom_call_target="tpu_custom_call" | custom-call | tf_op jit(solution)/shard_map/pallas_call | solution.py:506
